TPU v7x, 32 devices: a whole 2x2x4 slice. The times are simulated.
32 devices in a mesh: rows: 8 (over z, y), grp: 4 (over x, core).
Axes of the slice: x: 2, y: 2, z: 4, core: 2. Of those that a mesh axis runs over, the one named last changes fastest.
Arguments:
- features: float32 [8192, 128], P(('rows', 'grp'))
- key_ids: int32 [8192], P(('rows', 'grp')), may hold values from 0 to 23, as said below
- owner: int32 [24], replicated, may hold values from 0 to 23, each once
Outputs:
- covariance: float32 [3072, 128], P(('rows', 'grp'))
Inputs may be any that keep to these rules, and one draw needn't show every extreme that they name: `key_ids`: every key is the key of at least 2 rows.
All inputs are finite; a program needn't handle non-finite values.
Results may differ from a plain program's by a relative error of at most 0.0003.
Values sent between devices are 32-bit elements; how exact they have to be, the bound alone decides.
A program may use at most 64 MiB of HBM per device.

v0:
```python
import jax
import jax.numpy as jnp
from jax import lax
from jax.sharding import PartitionSpec as P


def local(features, key_ids, owner):
    nkeys = owner.shape[0]
    width = features.shape[1]
    labels = jnp.arange(nkeys, dtype=jnp.int32)
    member = key_ids[:, None] == labels[None, :]
    slot = jnp.sum(jnp.where(member, owner[None, :], 0), axis=1)
    onehot = (slot[:, None] == labels[None, :]).astype(jnp.float32)
    contract = (((0,), (0,)), ((), ()))
    local_total = lax.dot_general(
        onehot,
        features,
        contract,
        precision=lax.Precision.HIGHEST,
        preferred_element_type=jnp.float32,
    )
    local_count = jnp.sum(onehot, axis=0)
    weighted = (onehot[:, :, None] * features[:, None, :]).reshape(features.shape[0], nkeys * width)
    gram_flat = lax.dot_general(
        weighted,
        features,
        contract,
        precision=lax.Precision.HIGHEST,
        preferred_element_type=jnp.float32,
    )
    n_rows = lax.axis_size("rows")
    n_grp = lax.axis_size("grp")
    local_rows = nkeys * width // (n_rows * n_grp)
    partial_value = lax.psum_scatter(gram_flat, "rows", scatter_dimension=0, tiled=True)
    received = lax.psum_scatter(partial_value, "grp", scatter_dimension=0, tiled=True)
    position = lax.axis_index("rows") * n_grp + lax.axis_index("grp")
    base = position * local_rows
    target = base + jnp.arange(local_rows, dtype=jnp.int32)
    owner_slot = target // width
    column = target % width
    total, count = lax.psum((local_total, local_count), ("rows", "grp"))
    slot_total = jnp.take(total, owner_slot, axis=0)
    slot_count = jnp.take(count, owner_slot, axis=0)[:, None]
    own_total = jnp.take_along_axis(slot_total, column[:, None], axis=1)
    centred = received - own_total * slot_total / slot_count
    return centred / (slot_count - 1.0)


def solution(mesh):
    placed = (P(("rows", "grp"), None), P(("rows", "grp")), P())
    return jax.shard_map(
        local, mesh=mesh, in_specs=placed, out_specs=P(("rows", "grp"), None), check_vma=False
    )
```

profile of v0, /device:TPU:0, one launch (start us, length us, event | category | flops | bytes accessed | tf_op | source)
XLA Modules:
  0.0 113.6 jit_solution(11234650140521624888)
XLA Ops:
  6.5 0.0 copy-start
  6.5 0.0 reduce-scatter.3.cloned.1.call-start
  6.5 0.8 select_reduce_fusion
  7.4 0.1 copy.4
  7.5 1.8 %broadcast_multiply_fusion = f32[256,24,128]{2,1,0:T(8,128)S(1)} fusion(f32[256,128]{1,0:T(8,128)} %param.3, f32[256,24]{1,0:T(8,128)S(1)} %copy.4), kind=kLoop, calls=%fused_computation.6 | loop fusion | flops 786432 | bytes 3301376 | tf_op jit(solution)/shard_map/mul | solution.py:23
  9.3 0.0 copy-done
  9.3 6.2 %fusion = f32[3072,128]{1,0:T(8,128)} fusion(f32[256,128]{1,0:T(8,128)S(1)} %copy-done, f32[32,8,24,128]{3,2,1,0:T(8,128)S(1)} %bitcast.12), kind=kOutput, calls=%fused_computation.3 | convolution fusion | flops 1207959552 | bytes 4849664 | tf_op jit(solution)/shard_map/dot_general | solution.py:24
  15.5 0.0 reduce-scatter.3.cloned.1.call-update
  15.5 0.0 reduce-scatter.5.cloned.1.call-start
  15.6 0.1 fusion.6
  15.7 0.2 fusion.3
  15.8 42.8 %all-reduce = (f32[24,128]{1,0:T(8,128)S(1)}, f32[24]{0:T(128)S(1)}) all-reduce(f32[24,128]{1,0:T(8,128)S(1)} %fusion.3, f32[24]{0:T(128)S(1)} %fusion.6), channel_id=1, replica_groups=mesh['rows'=8,'grp'=4] {'rows','grp'}, use_global_device_ids=true, to_apply=%region_3.4 | all-reduce | flops 3096 | bytes 24768 | tf_op jit(solution)/shard_map/psum | solution.py:41
  58.6 1.2 %gather_fusion.1 = f32[96]{0:T(128)S(1)} fusion(f32[24]{0:T(128)S(1)} %get-tuple-element.6, s32[1024]{0:T(1024)S(1)} %pad_clamp_fusion), kind=kCustom, calls=%fused_computation.1 | custom fusion | bytes 1152 | tf_op jit(solution)/shard_map/jit(_take)/gather | solution.py:43
  59.9 0.6 gather_fusion
  60.6 0.1 broadcast_select_fusion
  60.6 23.5 %reduce-scatter.3.cloned.1.call-done = f32[384,128]{1,0:T(8,128)} async-done(((f32[3072,128]{1,0:T(8,128)}), f32[384,128]{1,0:T(8,128)}) %reduce-scatter.3.cloned.1.call-update) | async-done | bytes 196624 | tf_op jit(solution)/shard_map/reduce_scatter | solution.py:34
  84.1 0.0 reduce-scatter.5.cloned.1.call-update
  84.2 1.2 %gather_fusion.2 = f32[96]{0:T(128)S(1)} fusion(f32[96,128]{1,0:T(8,128)S(1)} %broadcast_select_fusion, s32[96]{0:T(128)S(1)} %or_bitcast_fusion), kind=kCustom, calls=%fused_computation.2 | custom fusion | bytes 1536 | tf_op jit(solution)/shard_map/jit(take_along_axis)/gather | solution.py:44
  85.4 19.8 %reduce-scatter.5.cloned.1.call-done = f32[96,128]{1,0:T(8,128)} async-done(((f32[384,128]{1,0:T(8,128)}), f32[96,128]{1,0:T(8,128)}) %reduce-scatter.5.cloned.1.call-update) | async-done | bytes 49168 | tf_op jit(solution)/shard_map/reduce_scatter | solution.py:35
  105.2 1.5 %subtract_divide_fusion = f32[96,128]{1,0:T(8,128)} fusion(f32[96,128]{1,0:T(8,128)} %reduce-scatter.5.cloned.1.call-done, f32[96]{0:T(128)S(1)} %get-tuple-element.7, f32[96]{0:T(128)S(1)} %get-tuple-element.8, f32[96]{0:T(128)S(1)} %get-tuple-element.9, f32[96,128]{1,0:T(8,128)S(1)} %gather_fusion, pred[96]{0:T(512)(128)(4,1)S(1)} %compare_and_fusion), kind=kLoop, calls=%fused_computation.7 | loop fusion | flops 61440 | bytes 148704 | tf_op jit(solution)/shard_map/div | solution.py:46
  (9 shorter events, 0.1 us)
Async XLA Ops:
  6.5 2.7 %copy-start = (f32[256,128]{1,0:T(8,128)S(1)}, f32[256,128]{1,0:T(8,128)}, u32[]{:S(2)}) copy-start(f32[256,128]{1,0:T(8,128)} %param.3) | copy-start | bytes 393220
  6.5 77.6 %reduce-scatter.3.cloned.1.call-start = ((), (), s32[]{:S(2)}) async-start(), calls=%async_computation.2 | async-start | bytes 1769472 | tf_op jit(solution)/shard_map/reduce_scatter | solution.py:34
  15.5 89.7 %reduce-scatter.5.cloned.1.call-start = ((), (), s32[]{:S(2)}) async-start(), calls=%async_computation.3 | async-start | bytes 245760 | tf_op jit(solution)/shard_map/reduce_scatter | solution.py:35
Sparse Core Ops, SparseCore 0:
  15.6 68.4 reduce-scatter.2
  86.6 18.5 reduce-scatter.4
where the time goes:
time: 114 us
  waiting for transfers between devices  43.3 us (38%)
  blocking collectives  42.8 us (38%)
  between operations  13.5 us (12%)
  matrix products  6.39 us (6%)
  other arithmetic  4.42 us (4%)
  local copies, waits for them, and re-layouts  3.2 us (3%)
    psum x1, blocking collectives, local(): total, count = lax.psum((local_total, local_count), ('rows', 'grp'))  42.8 us
    reduce_scatter x1, waiting for transfers between devices, local(): lax.psum_scatter(gram_flat, 'rows', scatter_dimension=0, tiled=True)  23.5 us
    reduce_scatter x1, waiting for transfers between devices, local(): lax.psum_scatter(partial_value, 'grp', scatter_dimension=0, tiled=True)  19.8 us
    dot_general x1, matrix products, local(): lax.dot_general(weighted, features, contract, precision=lax.Precision.HIG...  6.23 us
  transfers between devices with their start and end apart: 2, of which 2 were waited for; matrix products, arithmetic and copies ran while one was open for 3% of the time, Pallas kernels for 0%

commit v1 on v0

--- a/solution.py
+++ b/solution.py
@@ -38,7 +38,7 @@
     target = base + jnp.arange(local_rows, dtype=jnp.int32)
     owner_slot = target // width
     column = target % width
-    total, count = lax.psum((local_total, local_count), ("rows", "grp"))
+    total, count = lax.psum(lax.psum((local_total, local_count), "grp"), "rows")
     slot_total = jnp.take(total, owner_slot, axis=0)
     slot_count = jnp.take(count, owner_slot, axis=0)[:, None]
     own_total = jnp.take_along_axis(slot_total, column[:, None], axis=1)

time: 114 us -> 114 us (level)
  waiting for transfers between devices: 43.3 us -> 35.6 us
  blocking collectives: 42.8 us -> 50.3 us
    reduce_scatter x1, waiting for transfers between devices: 23.5 us -> 15.8 us  [local(): lax.psum_scatter(gram_flat, 'rows', scatter_dimension=0, tiled=True)]
    psum x1 -> x2, blocking collectives: 42.8 us -> 50.3 us  [local(): total, count = lax.psum(lax.psum((local_total, local_count), 'grp'), 'rows')]
where the time goes in v1:
time: 114 us; the launch traced here: 113 us
  blocking collectives  50.3 us (44%)
  waiting for transfers between devices  35.6 us (31%)
  between operations  13.5 us (12%)
  matrix products  6.39 us (6%)
  other arithmetic  4.42 us (4%)
  local copies, waits for them, and re-layouts  3.2 us (3%)
    psum x2, blocking collectives, local(): total, count = lax.psum(lax.psum((local_total, local_count), 'grp'), 'rows')  50.3 us
    reduce_scatter x1, waiting for transfers between devices, local(): lax.psum_scatter(partial_value, 'grp', scatter_dimension=0, tiled=True)  19.7 us
    reduce_scatter x1, waiting for transfers between devices, local(): lax.psum_scatter(gram_flat, 'rows', scatter_dimension=0, tiled=True)  15.8 us
    dot_general x1, matrix products, local(): lax.dot_general(weighted, features, contract, precision=lax.Precision.HIG...  6.23 us
  transfers between devices with their start and end apart: 2, of which 2 were waited for; matrix products, arithmetic and copies ran while one was open for 3% of the time, Pallas kernels for 0%

profile of v1, /device:TPU:0, one launch (start us, length us, event | category | flops | bytes accessed | tf_op | source)
XLA Modules:
  0.0 113.4 jit_solution(15934128024579430360)
XLA Ops:
  6.5 0.0 copy-start
  6.5 0.0 reduce-scatter.3.cloned.1.call-start
  6.5 0.8 select_reduce_fusion
  7.4 0.1 copy.4
  7.5 1.8 %broadcast_multiply_fusion = f32[256,24,128]{2,1,0:T(8,128)S(1)} fusion(f32[256,128]{1,0:T(8,128)} %param.3, f32[256,24]{1,0:T(8,128)S(1)} %copy.4), kind=kLoop, calls=%fused_computation.6 | loop fusion | flops 786432 | bytes 3301376 | tf_op jit(solution)/shard_map/mul | solution.py:23
  9.3 0.0 copy-done
  9.3 6.2 %fusion = f32[3072,128]{1,0:T(8,128)} fusion(f32[256,128]{1,0:T(8,128)S(1)} %copy-done, f32[32,8,24,128]{3,2,1,0:T(8,128)S(1)} %bitcast.12), kind=kOutput, calls=%fused_computation.3 | convolution fusion | flops 1207959552 | bytes 4849664 | tf_op jit(solution)/shard_map/dot_general | solution.py:24
  15.5 0.0 reduce-scatter.3.cloned.1.call-update
  15.5 0.0 reduce-scatter.5.cloned.1.call-start
  15.6 0.1 fusion.6
  15.7 0.2 fusion.3
  15.8 12.7 %all-reduce.1 = (f32[24,128]{1,0:T(8,128)S(1)}, f32[24]{0:T(128)S(1)}) all-reduce(f32[24,128]{1,0:T(8,128)S(1)} %fusion.3, f32[24]{0:T(128)S(1)} %fusion.6), channel_id=1, replica_groups=mesh['rows'=8,'grp'=4] {'grp'}, use_global_device_ids=true, to_apply=%region_3.4 | all-reduce | flops 3096 | bytes 24768 | tf_op jit(solution)/shard_map/psum | solution.py:41
  28.5 37.6 %all-reduce = (f32[24,128]{1,0:T(8,128)S(1)}, f32[24]{0:T(128)S(1)}) all-reduce(f32[24,128]{1,0:T(8,128)S(1)} %get-tuple-element.7, f32[24]{0:T(128)S(1)} %get-tuple-element.8), channel_id=1, replica_groups=mesh['rows'=8,'grp'=4] {'rows'}, use_global_device_ids=true, to_apply=%region_4.5 | all-reduce | flops 3096 | bytes 24768 | tf_op jit(solution)/shard_map/psum | solution.py:41
  66.2 1.2 %gather_fusion.1 = f32[96]{0:T(128)S(1)} fusion(f32[24]{0:T(128)S(1)} %get-tuple-element.6, s32[1024]{0:T(1024)S(1)} %pad_clamp_fusion), kind=kCustom, calls=%fused_computation.1 | custom fusion | bytes 1152 | tf_op jit(solution)/shard_map/jit(_take)/gather | solution.py:43
  67.4 0.6 gather_fusion
  68.1 0.1 broadcast_select_fusion
  68.2 15.8 %reduce-scatter.3.cloned.1.call-done = f32[384,128]{1,0:T(8,128)} async-done(((f32[3072,128]{1,0:T(8,128)}), f32[384,128]{1,0:T(8,128)}) %reduce-scatter.3.cloned.1.call-update) | async-done | bytes 196624 | tf_op jit(solution)/shard_map/reduce_scatter | solution.py:34
  84.0 0.0 reduce-scatter.5.cloned.1.call-update
  84.0 1.2 %gather_fusion.2 = f32[96]{0:T(128)S(1)} fusion(f32[96,128]{1,0:T(8,128)S(1)} %broadcast_select_fusion, s32[96]{0:T(128)S(1)} %or_bitcast_fusion), kind=kCustom, calls=%fused_computation.2 | custom fusion | bytes 1536 | tf_op jit(solution)/shard_map/jit(take_along_axis)/gather | solution.py:44
  85.3 19.7 %reduce-scatter.5.cloned.1.call-done = f32[96,128]{1,0:T(8,128)} async-done(((f32[384,128]{1,0:T(8,128)}), f32[96,128]{1,0:T(8,128)}) %reduce-scatter.5.cloned.1.call-update) | async-done | bytes 49168 | tf_op jit(solution)/shard_map/reduce_scatter | solution.py:35
  105.0 1.5 %subtract_divide_fusion = f32[96,128]{1,0:T(8,128)} fusion(f32[96,128]{1,0:T(8,128)} %reduce-scatter.5.cloned.1.call-done, f32[96]{0:T(128)S(1)} %get-tuple-element.9, f32[96]{0:T(128)S(1)} %get-tuple-element.10, f32[96]{0:T(128)S(1)} %get-tuple-element.11, f32[96,128]{1,0:T(8,128)S(1)} %gather_fusion, pred[96]{0:T(512)(128)(4,1)S(1)} %compare_and_fusion), kind=kLoop, calls=%fused_computation.7 | loop fusion | flops 61440 | bytes 148704 | tf_op jit(solution)/shard_map/div | solution.py:46
  (9 shorter events, 0.1 us)
Async XLA Ops:
  6.5 2.7 %copy-start = (f32[256,128]{1,0:T(8,128)S(1)}, f32[256,128]{1,0:T(8,128)}, u32[]{:S(2)}) copy-start(f32[256,128]{1,0:T(8,128)} %param.3) | copy-start | bytes 393220
  6.5 77.4 %reduce-scatter.3.cloned.1.call-start = ((), (), s32[]{:S(2)}) async-start(), calls=%async_computation.2 | async-start | bytes 1769472 | tf_op jit(solution)/shard_map/reduce_scatter | solution.py:34
  15.5 89.5 %reduce-scatter.5.cloned.1.call-start = ((), (), s32[]{:S(2)}) async-start(), calls=%async_computation.3 | async-start | bytes 245760 | tf_op jit(solution)/shard_map/reduce_scatter | solution.py:35
Sparse Core Ops, SparseCore 0:
  15.6 68.3 reduce-scatter.2
  86.4 18.5 reduce-scatter.4
